TPU v7x, 256 devices: a whole 4x4x8 slice. The times are simulated.
256 devices in a mesh: expert: 8 (over y, core), shard: 32 (over z, x).
Axes of the slice: x: 4, y: 4, z: 8, core: 2. Of those that a mesh axis runs over, the one named last changes fastest.
Arguments:
- master_gate: float32 [128, 2048, 768], P('expert', 'shard'), may hold values from -0.125 to 0.125
- second_gate: bfloat16 [128, 2048, 768], P('expert', 'shard'), may hold values from -0.0625 to 0.0625
- master_up: float32 [128, 2048, 768], P('expert', 'shard'), may hold values from -0.125 to 0.125
- second_up: bfloat16 [128, 2048, 768], P('expert', 'shard'), may hold values from -0.0625 to 0.0625
- router_weight: float32 [2048, 128], P('shard', 'expert'), may hold values from -0.125 to 0.125
- router_gain: float32 [2048], P('shard'), may hold values from 0.25 to 1.75
Outputs:
- final_gate: bfloat16 [128, 768, 2048], P('expert', 'shard')
- final_up: bfloat16 [128, 768, 2048], P('expert', 'shard')
- serve_router: bfloat16 [2048, 128], replicated
All inputs are finite; a program needn't handle non-finite values.
Results may differ from a plain program's by a relative error of at most 0.001.
Values may be sent and summed in bfloat16 or wider, within the bound.
A program may use at most 64 MiB of HBM per device.

v0:
```python
import jax
import jax.numpy as jnp
from jax import lax
from jax.sharding import Mesh
from jax.sharding import PartitionSpec as P

EXPERT = ("expert_0", "expert_1")


def laid_out(parts, dim):
    shape = list(parts.shape[1:])
    shape[dim] *= parts.shape[0]
    return jnp.moveaxis(parts, 0, dim).reshape(shape)


def copy_for_each(x, axis):
    copies = jnp.broadcast_to(x, (lax.axis_size(axis), *x.shape))
    return lax.all_to_all(copies, axis, split_axis=0, concat_axis=0, tiled=True)


def gathered_copies(x, axis, dim):
    return laid_out(copy_for_each(x, axis), dim)


def edges_of(length, count):
    turn = length // count
    if turn >= 8:
        turn -= turn % 8
    return [turn * k for k in range(1, count)]


def gather_in_order(x, axes, turns):
    parts = x
    for k in turns:
        parts = lax.all_gather(parts, axes[k])
    done = turns[::-1]
    back = [done.index(k) for k in range(len(axes))]
    parts = parts.transpose(*back, *range(len(axes), parts.ndim))
    return parts.reshape(-1, *x.shape)


def gather_all_axes(x, axes, dim):
    numbers = list(range(len(axes)))[::-1]
    cut = x.shape.index(max(x.shape[:-1] or x.shape))
    edges = [0, *edges_of(x.shape[cut], len(axes)), x.shape[cut]]
    gathered = []
    for k, (start, end) in enumerate(zip(edges, edges[1:])):
        if end > start:
            section = lax.slice_in_dim(x, start, end, axis=cut)
            gathered.append(gather_in_order(section, axes, numbers[k:] + numbers[:k]))
    return laid_out(jnp.concatenate(gathered, axis=cut + 1), dim)


def shards(master_gate, second_gate, master_up, second_up, router_weight, router_gain):
    merged_gate = master_gate + second_gate.astype(jnp.float32)
    merged_up = master_up + second_up.astype(jnp.float32)
    narrow_gate, narrow_up = (merged_gate.astype(jnp.bfloat16), merged_up.astype(jnp.bfloat16))
    final_gate, final_up = (
        lax.all_to_all(narrow_gate, "shard", split_axis=2, concat_axis=1, tiled=True),
        lax.all_to_all(narrow_up, "shard", split_axis=2, concat_axis=1, tiled=True),
    )
    final_gate = jnp.transpose(final_gate, (0, 2, 1))
    final_up = jnp.transpose(final_up, (0, 2, 1))
    part_router = (router_weight * router_gain[:, None]).astype(jnp.bfloat16)
    row_router = gathered_copies(part_router, "shard", 0)
    serve_router = gather_all_axes(row_router, EXPERT, 1)
    return (final_gate, final_up, serve_router)


def solution(mesh):
    split = Mesh(mesh.devices.reshape(4, 2, mesh.shape["shard"]), ("expert_0", "expert_1", "shard"))
    in_specs = (
        P(EXPERT, "shard", None),
        P(EXPERT, "shard", None),
        P(EXPERT, "shard", None),
        P(EXPERT, "shard", None),
        P("shard", EXPERT),
        P("shard"),
    )
    out_specs = (P(EXPERT, "shard", None), P(EXPERT, "shard", None), P())
    return jax.shard_map(
        shards, mesh=split, in_specs=in_specs, out_specs=out_specs, check_vma=False
    )
```

profile of v0, /device:TPU:6, one launch (start us, length us, event | category | flops | bytes accessed | tf_op | source)
XLA Modules:
  0.0 138.5 jit_solution(3208780866263310215)
XLA Ops:
  0.6 0.7 multiply_convert_fusion
  1.4 0.8 reshape.31
  2.1 11.6 %all-to-all-start.2 = ((bf16[32,2,512]{2,1,0:T(2,128)(2,1)}), bf16[32,2,512]{2,1,0:T(2,128)(2,1)S(1)}, u32[]{:S(2)}, u32[]{:S(2)}) async-start(bf16[32,2,512]{2,1,0:T(2,128)(2,1)} %reshape.31), calls=%async_computation.2 | async-start | bytes 131072 | tf_op jit(solution)/shard_map/all_to_all | solution.py:18
  13.7 3.9 %add_convert_fusion.1 = bf16[16,64,768]{2,1,0:T(8,128)(2,1)} fusion(f32[16,64,768]{2,1,0:T(8,128)} %param.6, bf16[16,64,768]{2,1,0:T(8,128)(2,1)} %param.7), kind=kLoop, calls=%fused_computation.1 | loop fusion | flops 2359296 | bytes 6291456 | tf_op jit(solution)/shard_map/convert_element_type | solution.py:57
  17.6 4.0 %copy.48 = bf16[16,64,768]{1,0,2:T(8,128)(2,1)S(1)} copy(bf16[16,64,768]{2,1,0:T(8,128)(2,1)} %add_convert_fusion.1) | data formatting | bytes 3145728 | tf_op jit(solution)/shard_map/convert_element_type | solution.py:57
  21.6 3.2 %reshape.27 = bf16[32,2,12288]{2,1,0:T(2,128)(2,1)} reshape(bf16[768,16,64]{2,1,0:T(8,128)(2,1)S(1)} %bitcast.34) | data formatting | bytes 3145728
  24.8 0.0 copy-start
  24.8 0.0 all-to-all-done.2
  24.8 10.1 %all-to-all-start = ((bf16[32,2,12288]{2,1,0:T(2,128)(2,1)}), bf16[32,2,12288]{2,1,0:T(2,128)(2,1)}, u32[]{:S(2)}, u32[]{:S(2)}) async-start(bf16[32,2,12288]{2,1,0:T(2,128)(2,1)} %reshape.27), calls=%async_computation | async-start | bytes 3145728 | tf_op jit(solution)/shard_map/all_to_all | solution.py:59
  34.9 0.0 copy-done
  34.9 3.0 %add_convert_fusion = bf16[16,64,768]{2,1,0:T(8,128)(2,1)} fusion(f32[16,64,768]{2,1,0:T(8,128)S(1)} %copy-done, bf16[16,64,768]{2,1,0:T(8,128)(2,1)} %param.9), kind=kLoop, calls=%fused_computation | loop fusion | flops 2359296 | bytes 6291456 | tf_op jit(solution)/shard_map/convert_element_type | solution.py:57
  37.9 4.0 %copy.51 = bf16[16,64,768]{1,0,2:T(8,128)(2,1)S(1)} copy(bf16[16,64,768]{2,1,0:T(8,128)(2,1)} %add_convert_fusion) | data formatting | bytes 3145728 | tf_op jit(solution)/shard_map/convert_element_type | solution.py:57
  41.9 3.2 %reshape.29 = bf16[32,2,12288]{2,1,0:T(2,128)(2,1)} reshape(bf16[768,16,64]{2,1,0:T(8,128)(2,1)S(1)} %bitcast.35) | data formatting | bytes 3145728
  45.1 28.6 %all-to-all-done = bf16[32,2,12288]{2,1,0:T(2,128)(2,1)} async-done(((bf16[32,2,12288]{2,1,0:T(2,128)(2,1)}), bf16[32,2,12288]{2,1,0:T(2,128)(2,1)}, u32[]{:S(2)}, u32[]{:S(2)}) %all-to-all-start) | async-done | bytes 1572896 | tf_op jit(solution)/shard_map/all_to_all | solution.py:59
  73.7 5.6 %all-to-all-start.1 = ((bf16[32,2,12288]{2,1,0:T(2,128)(2,1)}), bf16[32,2,12288]{2,1,0:T(2,128)(2,1)}, u32[]{:S(2)}, u32[]{:S(2)}) async-start(bf16[32,2,12288]{2,1,0:T(2,128)(2,1)} %reshape.29), calls=%async_computation.1 | async-start | bytes 3145728 | tf_op jit(solution)/shard_map/all_to_all | solution.py:60
  79.3 0.1 reshape.32
  79.5 0.1 all_gather.28
  79.6 12.7 %all_gather.29 = bf16[4,1024,16]{1,2,0:T(8,128)(2,1)S(1)} all-gather(bf16[1,1024,16]{1,2,0:T(8,128)(2,1)S(1)} %all_gather.28), channel_id=1, replica_groups=mesh['expert_0'=4,'expert_1'=2,'shard'=32] {'expert_0'}, dimensions={0}, use_global_device_ids=true | all-gather | bytes 163840 | tf_op jit(solution)/shard_map/all_gather | solution.py:35
  92.3 2.0 %all-gather.1 = bf16[8,1024,16]{1,2,0:T(8,128)(2,1)S(1)} all-gather(bf16[4,1024,16]{1,2,0:T(8,128)(2,1)S(1)} %all_gather.29), channel_id=3, replica_groups=mesh['expert_0'=4,'expert_1'=2,'shard'=32] {'expert_1'}, dimensions={0}, use_global_device_ids=true | all-gather | bytes 393216 | tf_op jit(solution)/shard_map/all_gather | solution.py:35
  94.3 0.1 all_gather.24
  94.5 1.9 %all_gather.25 = bf16[2,1024,16]{1,2,0:T(8,128)(2,1)S(1)} all-gather(bf16[1,1024,16]{1,2,0:T(8,128)(2,1)S(1)} %all_gather.24), channel_id=1, replica_groups=mesh['expert_0'=4,'expert_1'=2,'shard'=32] {'expert_1'}, dimensions={0}, use_global_device_ids=true | all-gather | bytes 98304 | tf_op jit(solution)/shard_map/all_gather | solution.py:35
  96.3 12.4 %all-gather = bf16[8,1024,16]{1,2,0:T(8,128)(2,1)S(1)} all-gather(bf16[2,1024,16]{1,2,0:T(8,128)(2,1)S(1)} %all_gather.25), channel_id=2, replica_groups=mesh['expert_0'=4,'expert_1'=2,'shard'=32] {'expert_0'}, dimensions={0}, use_global_device_ids=true | all-gather | bytes 327680 | tf_op jit(solution)/shard_map/all_gather | solution.py:35
  108.8 1.0 copy.57
  109.8 5.1 %reshape.28 = bf16[768,16,64]{2,1,0:T(8,128)(2,1)S(1)} reshape(bf16[32,2,12288]{2,1,0:T(2,128)(2,1)} %all-to-all-done) | data formatting | bytes 3145728
  114.9 3.7 %copy.50 = bf16[16,32,64,24]{2,1,3,0:T(8,128)(2,1)} copy(bf16[16,32,64,24]{2,0,3,1:T(8,128)(2,1)S(1)} %bitcast.36) | data formatting | bytes 3145728 | tf_op jit(solution)/shard_map/all_to_all | solution.py:59
  118.6 5.6 %all_to_all.32 = bf16[16,2048,24]{1,2,0:T(8,128)(2,1)} reshape(bf16[16,32,64,24]{2,1,3,0:T(8,128)(2,1)} %copy.50) | data formatting | bytes 3145728 | tf_op jit(solution)/shard_map/all_to_all | solution.py:59
  124.1 0.0 all-to-all-done.1
  124.1 5.1 %reshape.30 = bf16[768,16,64]{2,1,0:T(8,128)(2,1)S(1)} reshape(bf16[32,2,12288]{2,1,0:T(2,128)(2,1)} %all-to-all-done.1) | data formatting | bytes 3145728
  129.2 3.7 %copy.53 = bf16[16,32,64,24]{2,1,3,0:T(8,128)(2,1)} copy(bf16[16,32,64,24]{2,0,3,1:T(8,128)(2,1)S(1)} %bitcast.37) | data formatting | bytes 3145728 | tf_op jit(solution)/shard_map/all_to_all | solution.py:60
  132.9 5.6 %all_to_all.36 = bf16[16,2048,24]{1,2,0:T(8,128)(2,1)} reshape(bf16[16,32,64,24]{2,1,3,0:T(8,128)(2,1)} %copy.53) | data formatting | bytes 3145728 | tf_op jit(solution)/shard_map/all_to_all | solution.py:60
  (6 shorter events, 0.1 us)
Async XLA Ops:
  2.1 22.7 %all-to-all-start.2 = ((bf16[32,2,512]{2,1,0:T(2,128)(2,1)}), bf16[32,2,512]{2,1,0:T(2,128)(2,1)S(1)}, u32[]{:S(2)}, u32[]{:S(2)}) async-start(bf16[32,2,512]{2,1,0:T(2,128)(2,1)} %reshape.31), calls=%async_computation.2 | async-start | bytes 131072 | tf_op jit(solution)/shard_map/all_to_all | solution.py:18
  24.8 10.1 %copy-start = (f32[16,64,768]{2,1,0:T(8,128)S(1)}, f32[16,64,768]{2,1,0:T(8,128)}, u32[]{:S(2)}) copy-start(f32[16,64,768]{2,1,0:T(8,128)} %param.8) | copy-start | bytes 9437188
  24.8 48.9 %all-to-all-start = ((bf16[32,2,12288]{2,1,0:T(2,128)(2,1)}), bf16[32,2,12288]{2,1,0:T(2,128)(2,1)}, u32[]{:S(2)}, u32[]{:S(2)}) async-start(bf16[32,2,12288]{2,1,0:T(2,128)(2,1)} %reshape.27), calls=%async_computation | async-start | bytes 3145728 | tf_op jit(solution)/shard_map/all_to_all | solution.py:59
  73.7 50.4 %all-to-all-start.1 = ((bf16[32,2,12288]{2,1,0:T(2,128)(2,1)}), bf16[32,2,12288]{2,1,0:T(2,128)(2,1)}, u32[]{:S(2)}, u32[]{:S(2)}) async-start(bf16[32,2,12288]{2,1,0:T(2,128)(2,1)} %reshape.29), calls=%async_computation.1 | async-start | bytes 3145728 | tf_op jit(solution)/shard_map/all_to_all | solution.py:60
where the time goes:
time: 139 us; the launch traced here: 138 us
  local copies, waits for them, and re-layouts  45.3 us (33%)
  blocking collectives  28.9 us (21%)
  waiting for transfers between devices  28.6 us (21%)
  starting transfers between devices  27.3 us (20%)
  other arithmetic  7.6 us (5%)
    all_gather x4, blocking collectives, gather_in_order(): parts = lax.all_gather(parts, axes[k])  28.9 us
    all_to_all x1, waiting for transfers between devices, shards(): lax.all_to_all(narrow_gate, 'shard', split_axis=2, concat_axis=1, tiled=T...  28.6 us
    unnamed x10, local copies, waits for them, and re-layouts  18.5 us
    all_to_all x1, starting transfers between devices, copy_for_each(): return lax.all_to_all(copies, axis, split_axis=0, concat_axis=0, tiled=True)  11.6 us
    all_to_all x1, starting transfers between devices, shards(): lax.all_to_all(narrow_gate, 'shard', split_axis=2, concat_axis=1, tiled=T...  10.1 us
    all_to_all x2, local copies, waits for them, and re-layouts, shards(): lax.all_to_all(narrow_gate, 'shard', split_axis=2, concat_axis=1, tiled=T...  9.25 us
    all_to_all x2, local copies, waits for them, and re-layouts, shards(): lax.all_to_all(narrow_up, 'shard', split_axis=2, concat_axis=1, tiled=True)  9.25 us
    all_to_all x1, starting transfers between devices, shards(): lax.all_to_all(narrow_up, 'shard', split_axis=2, concat_axis=1, tiled=True)  5.61 us
  transfers between devices with their start and end apart: 3, of which 1 were waited for; matrix products, arithmetic and copies ran while one was open for 23% of the time, Pallas kernels for 0%

commit v1 on v0

--- a/solution.py
+++ b/solution.py
@@ -56,7 +56,12 @@
     merged_up = master_up + second_up.astype(jnp.float32)
     narrow_gate, narrow_up = (merged_gate.astype(jnp.bfloat16), merged_up.astype(jnp.bfloat16))
     final_gate, final_up = (
-        lax.all_to_all(narrow_gate, "shard", split_axis=2, concat_axis=1, tiled=True),
+        jnp.concatenate(
+            lax.all_to_all(
+                jnp.stack(jnp.split(narrow_gate, lax.axis_size("shard"), axis=2)), "shard", 0, 0
+            ),
+            axis=1,
+        ),
         lax.all_to_all(narrow_up, "shard", split_axis=2, concat_axis=1, tiled=True),
     )
     final_gate = jnp.transpose(final_gate, (0, 2, 1))

time: 139 us -> 141 us (1.014)
  local copies, waits for them, and re-layouts: 45.3 us -> 47.5 us
    unnamed x10 -> x43, local copies, waits for them, and re-layouts: 18.5 us -> 27.9 us
    all_to_all x2 -> x0, local copies, waits for them, and re-layouts: 9.25 us -> none  [shards(): lax.all_to_all(narrow_gate, 'shard', split_axis=2, concat_axis=1, tiled=T...]
    reshape x0 -> x3, local copies, waits for them, and re-layouts: none -> 5.97 us  [shards(): jnp.concatenate(lax.all_to_all(jnp.stack(jnp.split(narrow_gate, lax.axis_...]
    convert_element_type x1 -> x0, local copies, waits for them, and re-layouts: 4.02 us -> none  [shards(): merged_gate.astype(jnp.bfloat16)]
  transfers between devices with their start and end apart: 3 -> 3, of which waited for: 1 -> 1; matrix products, arithmetic and copies ran while one was open for 23% -> 28% of each run, Pallas kernels for 0% -> 0%
where the time goes in v1:
time: 141 us
  local copies, waits for them, and re-layouts  47.5 us (34%)
  blocking collectives  28.9 us (20%)
  waiting for transfers between devices  28.6 us (20%)
  starting transfers between devices  27.3 us (19%)
  other arithmetic  7.27 us (5%)
    all_gather x4, blocking collectives, gather_in_order(): parts = lax.all_gather(parts, axes[k])  28.9 us
    all_to_all x1, waiting for transfers between devices, shards(): lax.all_to_all(jnp.stack(jnp.split(narrow_gate, lax.axis_size('shard'), a...  28.6 us
    unnamed x43, local copies, waits for them, and re-layouts  27.9 us
    all_to_all x1, starting transfers between devices, copy_for_each(): return lax.all_to_all(copies, axis, split_axis=0, concat_axis=0, tiled=True)  11.6 us
    all_to_all x1, starting transfers between devices, shards(): lax.all_to_all(jnp.stack(jnp.split(narrow_gate, lax.axis_size('shard'), a...  10.1 us
    all_to_all x2, local copies, waits for them, and re-layouts, shards(): lax.all_to_all(narrow_up, 'shard', split_axis=2, concat_axis=1, tiled=True)  9.25 us
    reshape x3, local copies, waits for them, and re-layouts, shards(): jnp.concatenate(lax.all_to_all(jnp.stack(jnp.split(narrow_gate, lax.axis_...  5.97 us
    all_to_all x1, starting transfers between devices, shards(): lax.all_to_all(narrow_up, 'shard', split_axis=2, concat_axis=1, tiled=True)  5.61 us
  transfers between devices with their start and end apart: 3, of which 1 were waited for; matrix products, arithmetic and copies ran while one was open for 28% of the time, Pallas kernels for 0%

profile of v1, /device:TPU:6, one launch (start us, length us, event | category | flops | bytes accessed | tf_op | source)
XLA Modules:
  0.0 140.6 jit_solution(339826949255030993)
XLA Ops:
  0.6 0.7 multiply_convert_fusion
  1.4 0.8 reshape.39
  2.1 11.6 %all-to-all-start.2 = ((bf16[32,2,512]{2,1,0:T(2,128)(2,1)}), bf16[32,2,512]{2,1,0:T(2,128)(2,1)S(1)}, u32[]{:S(2)}, u32[]{:S(2)}) async-start(bf16[32,2,512]{2,1,0:T(2,128)(2,1)} %reshape.39), calls=%async_computation.2 | async-start | bytes 131072 | tf_op jit(solution)/shard_map/all_to_all | solution.py:18
  13.7 5.8 %copy.43 = f32[16,64,768]{1,2,0:T(8,128)} copy(f32[16,64,768]{2,1,0:T(8,128)} %param.6) | data formatting | bytes 6291456 | tf_op args[0]
  19.5 3.1 %copy.42 = bf16[16,64,768]{1,2,0:T(8,128)(2,1)S(1)} copy(bf16[16,64,768]{2,1,0:T(8,128)(2,1)} %param.7) | data formatting | bytes 3145728 | tf_op args[1]
  22.6 3.6 %add_convert_fusion = bf16[16,64,768]{1,2,0:T(8,128)(2,1)S(1)} fusion(f32[16,64,768]{1,2,0:T(8,128)} %copy.43, bf16[16,64,768]{1,2,0:T(8,128)(2,1)S(1)} %copy.42), kind=kLoop, calls=%fused_computation | loop fusion | flops 2359296 | bytes 6291456 | tf_op jit(solution)/shard_map/convert_element_type | solution.py:57
  27.0 3.2 %reshape.35 = bf16[32,2,12288]{2,1,0:T(2,128)(2,1)} reshape(bf16[32,16,24,64]{3,2,1,0:T(8,128)(2,1)S(1)} %bitcast.164) | data formatting | bytes 3145728
  30.1 0.0 copy-start
  30.1 0.0 all-to-all-done.2
  30.1 10.1 %all-to-all-start = ((bf16[32,2,12288]{2,1,0:T(2,128)(2,1)}), bf16[32,2,12288]{2,1,0:T(2,128)(2,1)}, u32[]{:S(2)}, u32[]{:S(2)}) async-start(bf16[32,2,12288]{2,1,0:T(2,128)(2,1)} %reshape.35), calls=%async_computation | async-start | bytes 3145728 | tf_op jit(solution)/shard_map/all_to_all | solution.py:60
  40.2 0.0 copy-done
  40.2 3.0 %add_convert_fusion.1 = bf16[16,64,768]{2,1,0:T(8,128)(2,1)} fusion(f32[16,64,768]{2,1,0:T(8,128)S(1)} %copy-done, bf16[16,64,768]{2,1,0:T(8,128)(2,1)} %param.9), kind=kLoop, calls=%fused_computation.1 | loop fusion | flops 2359296 | bytes 6291456 | tf_op jit(solution)/shard_map/convert_element_type | solution.py:57
  43.2 4.0 %copy.45 = bf16[16,64,768]{1,0,2:T(8,128)(2,1)S(1)} copy(bf16[16,64,768]{2,1,0:T(8,128)(2,1)} %add_convert_fusion.1) | data formatting | bytes 3145728 | tf_op jit(solution)/shard_map/convert_element_type | solution.py:57
  47.2 3.2 %reshape.37 = bf16[32,2,12288]{2,1,0:T(2,128)(2,1)} reshape(bf16[768,16,64]{2,1,0:T(8,128)(2,1)S(1)} %bitcast.162) | data formatting | bytes 3145728
  50.4 28.6 %all-to-all-done = bf16[32,2,12288]{2,1,0:T(2,128)(2,1)} async-done(((bf16[32,2,12288]{2,1,0:T(2,128)(2,1)}), bf16[32,2,12288]{2,1,0:T(2,128)(2,1)}, u32[]{:S(2)}, u32[]{:S(2)}) %all-to-all-start) | async-done | bytes 1572896 | tf_op jit(solution)/shard_map/all_to_all | solution.py:60
  79.0 5.6 %all-to-all-start.1 = ((bf16[32,2,12288]{2,1,0:T(2,128)(2,1)}), bf16[32,2,12288]{2,1,0:T(2,128)(2,1)}, u32[]{:S(2)}, u32[]{:S(2)}) async-start(bf16[32,2,12288]{2,1,0:T(2,128)(2,1)} %reshape.37), calls=%async_computation.1 | async-start | bytes 3145728 | tf_op jit(solution)/shard_map/all_to_all | solution.py:65
  84.7 0.1 reshape.40
  84.8 0.1 all_gather.28
  85.0 12.7 %all_gather.29 = bf16[4,1024,16]{1,2,0:T(8,128)(2,1)S(1)} all-gather(bf16[1,1024,16]{1,2,0:T(8,128)(2,1)S(1)} %all_gather.28), channel_id=1, replica_groups=mesh['expert_0'=4,'expert_1'=2,'shard'=32] {'expert_0'}, dimensions={0}, use_global_device_ids=true | all-gather | bytes 163840 | tf_op jit(solution)/shard_map/all_gather | solution.py:35
  97.6 2.0 %all-gather.1 = bf16[8,1024,16]{1,2,0:T(8,128)(2,1)S(1)} all-gather(bf16[4,1024,16]{1,2,0:T(8,128)(2,1)S(1)} %all_gather.29), channel_id=3, replica_groups=mesh['expert_0'=4,'expert_1'=2,'shard'=32] {'expert_1'}, dimensions={0}, use_global_device_ids=true | all-gather | bytes 393216 | tf_op jit(solution)/shard_map/all_gather | solution.py:35
  99.7 0.1 all_gather.24
  99.8 1.9 %all_gather.25 = bf16[2,1024,16]{1,2,0:T(8,128)(2,1)S(1)} all-gather(bf16[1,1024,16]{1,2,0:T(8,128)(2,1)S(1)} %all_gather.24), channel_id=1, replica_groups=mesh['expert_0'=4,'expert_1'=2,'shard'=32] {'expert_1'}, dimensions={0}, use_global_device_ids=true | all-gather | bytes 98304 | tf_op jit(solution)/shard_map/all_gather | solution.py:35
  101.6 12.4 %all-gather = bf16[8,1024,16]{1,2,0:T(8,128)(2,1)S(1)} all-gather(bf16[2,1024,16]{1,2,0:T(8,128)(2,1)S(1)} %all_gather.25), channel_id=2, replica_groups=mesh['expert_0'=4,'expert_1'=2,'shard'=32] {'expert_0'}, dimensions={0}, use_global_device_ids=true | all-gather | bytes 327680 | tf_op jit(solution)/shard_map/all_gather | solution.py:35
  114.1 1.0 copy.51
  115.1 5.1 %reshape.36 = bf16[32,16,24,64]{3,2,1,0:T(8,128)(2,1)S(1)} reshape(bf16[32,2,12288]{2,1,0:T(2,128)(2,1)} %all-to-all-done) | data formatting | bytes 3145728
  120.2 0.5 bitcast_bitcast_fusion
  120.8 2.0 %copy.44 = bf16[16,32,64,24]{2,1,3,0:T(8,128)(2,1)S(1)} copy(bf16[16,32,64,24]{2,3,0,1:T(8,128)(2,1)S(1)} %bitcast_bitcast_fusion) | data formatting | bytes 3145728 | tf_op jit(solution)/shard_map/reshape | solution.py:59
  122.8 3.4 %reshape.28 = bf16[16,2048,24]{1,2,0:T(8,128)(2,1)} reshape(bf16[16,32,64,24]{2,1,3,0:T(8,128)(2,1)S(1)} %copy.44) | data formatting | bytes 3145728 | tf_op jit(solution)/shard_map/reshape | solution.py:59
  126.2 0.0 all-to-all-done.1
  126.2 5.1 %reshape.38 = bf16[768,16,64]{2,1,0:T(8,128)(2,1)S(1)} reshape(bf16[32,2,12288]{2,1,0:T(2,128)(2,1)} %all-to-all-done.1) | data formatting | bytes 3145728
  131.3 3.7 %copy.47 = bf16[16,32,64,24]{2,1,3,0:T(8,128)(2,1)} copy(bf16[16,32,64,24]{2,0,3,1:T(8,128)(2,1)S(1)} %bitcast.163) | data formatting | bytes 3145728 | tf_op jit(solution)/shard_map/all_to_all | solution.py:65
  135.0 5.6 %all_to_all.23 = bf16[16,2048,24]{1,2,0:T(8,128)(2,1)} reshape(bf16[16,32,64,24]{2,1,3,0:T(8,128)(2,1)} %copy.47) | data formatting | bytes 3145728 | tf_op jit(solution)/shard_map/all_to_all | solution.py:65
  (38 shorter events, 0.7 us)
Async XLA Ops:
  2.1 28.0 %all-to-all-start.2 = ((bf16[32,2,512]{2,1,0:T(2,128)(2,1)}), bf16[32,2,512]{2,1,0:T(2,128)(2,1)S(1)}, u32[]{:S(2)}, u32[]{:S(2)}) async-start(bf16[32,2,512]{2,1,0:T(2,128)(2,1)} %reshape.39), calls=%async_computation.2 | async-start | bytes 131072 | tf_op jit(solution)/shard_map/all_to_all | solution.py:18
  30.1 10.1 %copy-start = (f32[16,64,768]{2,1,0:T(8,128)S(1)}, f32[16,64,768]{2,1,0:T(8,128)}, u32[]{:S(2)}) copy-start(f32[16,64,768]{2,1,0:T(8,128)} %param.8) | copy-start | bytes 9437188
  30.1 48.9 %all-to-all-start = ((bf16[32,2,12288]{2,1,0:T(2,128)(2,1)}), bf16[32,2,12288]{2,1,0:T(2,128)(2,1)}, u32[]{:S(2)}, u32[]{:S(2)}) async-start(bf16[32,2,12288]{2,1,0:T(2,128)(2,1)} %reshape.35), calls=%async_computation | async-start | bytes 3145728 | tf_op jit(solution)/shard_map/all_to_all | solution.py:60
  79.0 47.2 %all-to-all-start.1 = ((bf16[32,2,12288]{2,1,0:T(2,128)(2,1)}), bf16[32,2,12288]{2,1,0:T(2,128)(2,1)}, u32[]{:S(2)}, u32[]{:S(2)}) async-start(bf16[32,2,12288]{2,1,0:T(2,128)(2,1)} %reshape.37), calls=%async_computation.1 | async-start | bytes 3145728 | tf_op jit(solution)/shard_map/all_to_all | solution.py:65
